TPU v7x, 512 devices: a whole 4x8x8 slice. The times are simulated.
512 devices in a mesh: gz: 256 (over x, z, y), col: 2 (over core).
Axes of the slice: x: 4, y: 8, z: 8, core: 2. Of those that a mesh axis runs over, the one named last changes fastest.
Arguments:
- velocity: float32 [1024, 3, 128, 128], P('gz', None, 'col'), may hold values from -6 to 6
- forces: float32 [3, 2097152], P(None, ('gz', 'col')), may hold values from -60 to 60
- offsets: float32 [3, 2097152], P(None, ('gz', 'col')), may hold values from 0 to 1
- cell_x: int32 [2097152], P(('gz', 'col')), may hold values from 0 to 127
- cell_y: int32 [2097152], P(('gz', 'col')), may hold values from 0 to 127
- cell_z: int32 [2097152], P(('gz', 'col')), may hold values from 0 to 12
- band_start: int32 [256], P('gz'), may hold values from 0 to 255, as said below
Outputs:
- force_field: float32 [1024, 3, 128, 128], P('gz', None, 'col')
- velocity_next: float32 [1024, 3, 128, 128], P('gz', None, 'col')
Inputs may be any that keep to these rules, and one draw needn't show every extreme that they name: (g - band_start[g]) mod 256 lies in 0 to 3 for every gz index g.
All inputs are finite; a program needn't handle non-finite values.
Results may differ from a plain program's by a relative error of at most 0.0037.
Values sent between devices are 32-bit elements; how exact they have to be, the bound alone decides.
No kernel may reach another device: no remote copies, remote signals or barrier semaphores. Data moves between devices by JAX's collectives and lax.ppermute only.
A program may use at most 64 MiB of HBM per device.

v0:
```python
import jax
import jax.numpy as jnp
from jax import lax
from jax.experimental import pallas as pl
from jax.experimental.pallas import tpu as pltpu
from jax.sharding import PartitionSpec as P

viscous = 0.15
ROWS = 32
ATTRS = 9
LIST = ROWS * ATTRS
KROWS = 16
KERNEL_VMEM = 16 << 20
SLOTS = 24
TILE = 16


def vmem():
    return pl.BlockSpec(memory_space=pltpu.VMEM)


def smem():
    return pl.BlockSpec(memory_space=pltpu.SMEM)


def corner_weights(t):
    q = jnp.sqrt(1.0 + 4.0 * t - 4.0 * t * t)
    return (
        (3.0 - 2.0 * t - q) / 8.0,
        (3.0 - 2.0 * t + q) / 8.0,
        (1.0 + 2.0 * t + q) / 8.0,
        (1.0 + 2.0 * t - q) / 8.0,
    )


def in_vmem(x):
    return pltpu.with_memory_space_constraint(x, pltpu.VMEM)


def from_plane(list_ref, n, first_plane, span_z):
    rel = list_ref[pl.ds(n * LIST + 8 * ROWS, ROWS), :] - first_plane
    half = float(span_z // 2)
    rel = jnp.where(rel >= half, rel - float(span_z), rel)
    return jnp.where(rel < -half, rel + float(span_z), rel)


def prepare(list_ref, n, first_plane, dims, rows_ref):
    depth, span_x, span_y, span_z = dims

    def attr(a):
        return list_ref[pl.ds(n * LIST + a * ROWS, ROWS), :]

    def put(slot, value):
        rows_ref[pl.ds((n * SLOTS + slot) * ROWS, ROWS), :] = value

    def along(slot, cell, weights, span):
        tile = jnp.floor(cell * (1.0 / TILE))
        low = cell - tile * float(TILE)
        for b in range(4):
            at = low + float(b)
            put(slot + b, jnp.where(at >= float(TILE), at - float(TILE), at))
            put(slot + 4 + b, weights[b])
        put(slot + 8, tile)
        put(slot + 9, jnp.where(tile >= float(span // TILE - 1), 0.0, tile + 1.0))

    along(0, attr(6), corner_weights(attr(3)), span_x)
    rounded = [w.astype(jnp.bfloat16).astype(jnp.float32) for w in corner_weights(attr(4))]
    along(10, attr(7), rounded, span_y)
    wz = corner_weights(attr(5))
    rel = from_plane(list_ref, n, first_plane, span_z)
    for z in range(depth):
        plane = jnp.zeros_like(rel)
        for a in range(4):
            plane = jnp.where(rel == float(z - a), wz[a], plane)
        put(20 + z, plane)


def build(list_ref, rows_ref, turn, dims, a_ref, b_ref):
    depth, span_x, span_y, _ = dims
    per_list = ROWS // KROWS
    n = turn // per_list
    row = (turn % per_list) * KROWS
    row_at = lax.broadcasted_iota(jnp.int32, (TILE, 128), 0).astype(jnp.float32)
    nothing = jnp.zeros((TILE, 128), jnp.bfloat16)
    for r in range(KROWS):
        lanes = pl.ds(r * 128, 128)

        def get(slot):
            return rows_ref[pl.ds((n * SLOTS + slot) * ROWS + row + r, 1), :]

        def pattern(slot):
            weights = jnp.zeros((TILE, 128), jnp.float32)
            for b in range(4):
                weights = jnp.where(row_at == get(slot + b), get(slot + 4 + b), weights)
            tiles = jnp.where(row_at >= get(slot), get(slot + 8), get(slot + 9))
            return weights, tiles.astype(jnp.bfloat16)

        wx, x_tile = pattern(0)
        forces = [list_ref[pl.ds(n * LIST + c * ROWS + row + r, 1), :] for c in range(3)]
        a_rows = [(wx * f).astype(jnp.bfloat16) for f in forces]
        for t in range(span_x // TILE):
            here = x_tile == jnp.bfloat16(t)
            for c in range(3):
                a_ref[pl.ds(c * span_x + t * TILE, TILE), lanes] = jnp.where(here, a_rows[c], nothing)
        wy, y_tile = pattern(10)
        b_rows = [(wy * get(20 + z)).astype(jnp.bfloat16) for z in range(depth)]
        for t in range(span_y // TILE):
            here = y_tile == jnp.bfloat16(t)
            for z in range(depth):
                b_ref[pl.ds(z * span_y + t * TILE, TILE), lanes] = jnp.where(here, b_rows[z], nothing)


def spread_lists(list_ref, lists, first_plane, acc_ref, dims, rows_ref):
    depth, span_x, span_y, _ = dims
    a = pltpu.VMEM((3 * span_x, KROWS * 128), jnp.bfloat16)
    b = pltpu.VMEM((depth * span_y, KROWS * 128), jnp.bfloat16)

    def run(a0, b0, a1, b1):
        spread_turns(list_ref, lists, first_plane, acc_ref, dims, rows_ref, ((a0, b0), (a1, b1)))

    touch = jnp.zeros((ROWS, 128), jnp.float32)
    for n in range(lists):
        rel = from_plane(list_ref, n, first_plane, dims[3])
        touch = jnp.where(jnp.logical_and(rel > -4.0, rel < float(depth)), 1.0, touch)

    @pl.when(jnp.max(touch) > 0.0)
    def _():
        pl.run_scoped(run, a, b, a, b)


def spread_turns(list_ref, lists, first_plane, acc_ref, dims, rows_ref, bufs):
    depth, span_x, span_y, _ = dims
    turns = lists * (ROWS // KROWS)
    for n in range(lists):
        prepare(list_ref, n, first_plane, dims, rows_ref)

    def fill(turn, which):
        build(list_ref, rows_ref, turn, dims, *bufs[which])

    def add(which):
        a_ref, b_ref = bufs[which]
        out = lax.dot_general(
            a_ref[...], b_ref[...], (((1,), (1,)), ((), ())), preferred_element_type=jnp.float32
        )
        for z in range(depth):
            acc_ref[z] += out[:, z * span_y : (z + 1) * span_y]

    fill(0, 0)

    def two_turns(i, carry):
        fill(2 * i + 1, 1)
        add(0)
        fill(jnp.minimum(2 * i + 2, turns - 1), 0)
        add(1)
        return carry

    lax.fori_loop(0, turns // 2, two_turns, 0)


def scratch(lists):
    return [pltpu.VMEM((lists * SLOTS * ROWS, 128), jnp.float32)]


def cost(lists, dims):
    depth, span_x, span_y, _ = dims
    return pl.CostEstimate(
        flops=lists * ROWS * 128 * 3 * span_x * depth * span_y * 2,
        bytes_accessed=2000000,
        transcendentals=0,
    )


def own_plane(depth):
    return (lax.axis_index("gz") * depth).astype(jnp.float32)


def spread(markers, lists, acc, dims):
    depth, span_x, span_y, _ = dims

    def kernel(*refs):
        if acc is None:
            list_ref, out_ref, rows_ref = refs
            out_ref[...] = jnp.zeros_like(out_ref)
        else:
            list_ref, _, out_ref, rows_ref = refs
        spread_lists(list_ref, lists, own_plane(depth), out_ref, dims, rows_ref)

    operands = (in_vmem(markers),)
    if acc is not None:
        operands += (in_vmem(acc),)
    return pl.pallas_call(
        kernel,
        out_shape=pltpu.VMEM((depth, 3 * span_x, span_y), jnp.float32),
        in_specs=[vmem()] * len(operands),
        out_specs=vmem(),
        input_output_aliases={} if acc is None else {1: 0},
        scratch_shapes=scratch(lists),
        cost_estimate=cost(lists, dims),
        compiler_params=pltpu.CompilerParams(vmem_limit_bytes=KERNEL_VMEM),
        name="spread",
    )(*operands)


def spread_last(markers, lists, acc, planes, planes_at, dims):
    depth, span_x, span_y, _ = dims
    half = span_x // 2
    rows = depth * 3 * half

    def kernel(list_ref, in_ref, planes_ref, keep_ref, give_ref, acc_ref, rows_ref):
        acc_ref[...] = in_ref[...]
        give_ref[pl.ds(rows, 3 * half), :] = planes_ref[pl.ds(planes_at + 3 * half, 3 * half), :]
        spread_lists(list_ref, lists, own_plane(depth), acc_ref, dims, rows_ref)
        col = lax.axis_index("col")
        mine = pl.multiple_of(col * half, half)
        other = pl.multiple_of((1 - col) * half, half)
        for z in range(depth):
            for c in range(3):
                at = pl.ds((z * 3 + c) * half, half)
                keep_ref[at, :] = acc_ref[z, pl.ds(c * span_x + mine, half), :]
                give_ref[at, :] = acc_ref[z, pl.ds(c * span_x + other, half), :]

    return pl.pallas_call(
        kernel,
        out_shape=(
            pltpu.VMEM((rows, span_y), jnp.float32),
            pltpu.VMEM((rows + 3 * half, span_y), jnp.float32),
        ),
        in_specs=[vmem(), vmem(), vmem()],
        out_specs=(vmem(), vmem()),
        scratch_shapes=[pltpu.VMEM((depth, 3 * span_x, span_y), jnp.float32)] + scratch(lists),
        cost_estimate=cost(lists, dims),
        compiler_params=pltpu.CompilerParams(vmem_limit_bytes=KERNEL_VMEM),
        name="spread_last",
    )(in_vmem(markers), in_vmem(acc), in_vmem(planes))


def viscous_part(velocity, both):
    depth, _, half, span_y = velocity.shape
    low_at = LIST + 3 * half

    def kernel(v_ref, both_ref, base_ref):
        col = lax.axis_index("col")
        row_at = lax.broadcasted_iota(jnp.int32, (half, span_y), 0)
        for z in range(depth):
            for c in range(3):
                v = v_ref[z, c]
                x_low = both_ref[1 - col, pl.ds(low_at + z * 3 + c, 1), :]
                x_high = both_ref[1 - col, pl.ds(low_at + 3 * depth + z * 3 + c, 1), :]
                near = jnp.where(row_at == 0, x_high, pltpu.roll(v, 1, 0))
                near = near + jnp.where(row_at == half - 1, x_low, pltpu.roll(v, half - 1, 0))
                near = near + pltpu.roll(v, 1, 1) + pltpu.roll(v, span_y - 1, 1)
                if z > 0:
                    near = near + v_ref[z - 1, c]
                if z < depth - 1:
                    near = near + v_ref[z + 1, c]
                base_ref[z, c] = v + viscous * (near - 6.0 * v)

    return pl.pallas_call(
        kernel,
        out_shape=pltpu.VMEM(velocity.shape, jnp.float32),
        in_specs=[vmem(), vmem()],
        out_specs=vmem(),
        cost_estimate=pl.CostEstimate(flops=4000000, bytes_accessed=2000000, transcendentals=0),
        compiler_params=pltpu.CompilerParams(vmem_limit_bytes=KERNEL_VMEM),
        name="viscous_part",
    )(in_vmem(velocity), in_vmem(both))


def finish(keep, given, base, planes, planes_at):
    depth, _, half, span_y = base.shape
    rows = depth * 3 * half

    def kernel(keep_ref, given_ref, base_ref, planes_ref, force_hbm, next_hbm, force_ref, next_ref, sems):
        col = lax.axis_index("col")
        mine_at = jnp.where(col == 0, 0, depth - 1)
        copies = []
        for z in range(depth):
            mine = jnp.where(mine_at == z, viscous, 0.0)
            other = jnp.where(depth - 1 - mine_at == z, viscous, 0.0)
            for c in range(3):
                here = pl.ds((z * 3 + c) * half, half)
                force = keep_ref[here, :] + given_ref[1 - col, here, :]
                force_ref[z, c] = force
                base = base_ref[z, c]
                if z == 0 or z == depth - 1:
                    base = base + mine * planes_ref[pl.ds(planes_at + c * half, half), :]
                    base = base + other * given_ref[1 - col, pl.ds(rows + c * half, half), :]
                next_ref[z, c] = base + force
            copies.append(pltpu.make_async_copy(force_ref.at[z], force_hbm.at[z], sems.at[0, z]))
            copies.append(pltpu.make_async_copy(next_ref.at[z], next_hbm.at[z], sems.at[1, z]))
            copies[-2].start()
            copies[-1].start()
        for copy in copies:
            copy.wait()

    out = jax.ShapeDtypeStruct(base.shape, jnp.float32)
    return pl.pallas_call(
        kernel,
        out_shape=(out, out),
        in_specs=[vmem()] * 4,
        out_specs=(pl.BlockSpec(memory_space=pl.ANY), pl.BlockSpec(memory_space=pl.ANY)),
        scratch_shapes=[
            pltpu.VMEM(base.shape, jnp.float32),
            pltpu.VMEM(base.shape, jnp.float32),
            pltpu.SemaphoreType.DMA((2, depth)),
        ],
        compiler_params=pltpu.CompilerParams(vmem_limit_bytes=KERNEL_VMEM),
        name="finish",
    )(in_vmem(keep), in_vmem(given), in_vmem(base), in_vmem(planes))


def pack(velocity, forces, offsets, cell_x, cell_y, cell_z, band_start):
    depth, _, half, span_y = velocity.shape
    plane_rows = 3 * half
    total = LIST + plane_rows + 6 * depth

    def kernel(start_ref, v_ref, f_ref, o_ref, x_ref, y_ref, z_ref, sent_ref, plane_ref):
        for k in range(ROWS):
            for c in range(3):
                sent_ref[pl.ds(c * ROWS + k, 1), :] = f_ref[pl.ds(c, 1), pl.ds(k * 128, 128)]
                sent_ref[pl.ds((3 + c) * ROWS + k, 1), :] = o_ref[pl.ds(c, 1), pl.ds(k * 128, 128)]
        sent_ref[pl.ds(6 * ROWS, ROWS), :] = x_ref[...].astype(jnp.float32)
        sent_ref[pl.ds(7 * ROWS, ROWS), :] = y_ref[...].astype(jnp.float32)
        sent_ref[pl.ds(8 * ROWS, ROWS), :] = (z_ref[...] + start_ref[0] * depth).astype(jnp.float32)
        to_core = jnp.where(lax.axis_index("col") == 0, 0, depth - 1)
        for c in range(3):
            sent_ref[pl.ds(LIST + c * half, half), :] = v_ref[to_core, c]
            plane_ref[pl.ds(c * half, half), :] = v_ref[depth - 1 - to_core, c]
        for z in range(depth):
            for c in range(3):
                at = LIST + plane_rows + z * 3 + c
                sent_ref[pl.ds(at, 1), :] = v_ref[z, c, pl.ds(0, 1), :]
                sent_ref[pl.ds(at + 3 * depth, 1), :] = v_ref[z, c, pl.ds(half - 1, 1), :]

    return pl.pallas_call(
        kernel,
        out_shape=(
            pltpu.VMEM((total, span_y), jnp.float32),
            pltpu.VMEM((plane_rows, span_y), jnp.float32),
        ),
        in_specs=[smem()] + [vmem()] * 6,
        out_specs=(vmem(), vmem()),
        name="pack",
    )(
        band_start,
        velocity,
        forces,
        offsets,
        cell_x.reshape(ROWS, 128),
        cell_y.reshape(ROWS, 128),
        cell_z.reshape(ROWS, 128),
    )


def by_core(x, gz_count, by):
    pairs = []
    for g in range(gz_count):
        pairs.append((2 * g, 2 * ((g + by) % gz_count)))
        pairs.append((2 * g + 1, 2 * ((g - by) % gz_count) + 1))
    return lax.ppermute(x, ("gz", "col"), pairs)


def on_device(velocity, forces, offsets, cell_x, cell_y, cell_z, band_start):
    depth, _, half_x, span_y = velocity.shape
    gz_count = lax.axis_size("gz")
    col = lax.axis_index("col")
    span_x = half_x * lax.axis_size("col")
    dims = (depth, span_x, span_y, gz_count * depth)
    plane_rows = 3 * half_x
    sent, mine_out = pack(velocity, forces, offsets, cell_x, cell_y, cell_z, band_start)
    both = lax.all_gather(sent, "col", axis=0, tiled=False)
    chip = both[:, :LIST].reshape(2 * LIST, 128)
    partner = lax.dynamic_index_in_dim(both[:, LIST : LIST + plane_rows], 1 - col, 0, keepdims=False)

    second = by_core(chip, gz_count, 2)
    nearest = by_core(jnp.concatenate([chip, mine_out, partner]), gz_count, 1)
    acc = spread(sent, 1, None, dims)
    third = by_core(second, gz_count, 1)
    acc = spread(second, 2, acc, dims)
    acc = spread(nearest, 2, acc, dims)
    keep, give = spread_last(third, 2, acc, nearest, 2 * LIST, dims)
    given = lax.all_gather(give, "col", axis=0, tiled=False)
    base = viscous_part(velocity, both)
    return finish(keep, given, base, nearest, 2 * LIST)


def solution(mesh):
    in_specs = (
        P("gz", None, "col", None),
        P(None, ("gz", "col")),
        P(None, ("gz", "col")),
        P(("gz", "col")),
        P(("gz", "col")),
        P(("gz", "col")),
        P("gz"),
    )
    out_specs = (P("gz", None, "col", None), P("gz", None, "col", None))
    return jax.shard_map(
        on_device, mesh=mesh, in_specs=in_specs, out_specs=out_specs, check_vma=False
    )
```

profile of v0, /device:TPU:1, one launch (start us, length us, event | category | flops | bytes accessed | tf_op | source)
XLA Modules:
  0.0 48.1 jit_solution(12573969593212083494)
XLA Ops:
  1.3 1.2 %pack.1 = (f32[504,128]{1,0:T(8,128)S(1)}, f32[192,128]{1,0:T(8,128)S(1)}) custom-call(s32[1]{0:T(128)S(6)} %copy.13.start_ref, f32[4,3,64,128]{3,2,1,0:T(8,128)} %v_ref.3, f32[3,4096]{1,0:T(4,128)} %f_ref.1, f32[3,4096]{1,0:T(4,128)} %o_ref.1, s32[32,128]{1,0:T(8,128)} %bitcast.14, s32[32,128]{1,0:T(8,128)} %bitcast.15, s32[32,128]{1,0:T(8,128)} %bitcast.16), custom_call_target="tpu_custom_call" | custom-call | tf_op jit(solution)/shard_map/pack/pallas_call | solution.py:335
  2.4 8.6 %all-gather = f32[1008,128]{1,0:T(8,128)S(1)} all-gather(f32[504,128]{1,0:T(8,128)S(1)} %get-tuple-element.6.refs_0_), channel_id=2, replica_groups=mesh['gz'=256,'col'=2] {'col'}, dimensions={0}, use_global_device_ids=true | all-gather | bytes 774144 | tf_op jit(solution)/shard_map/all_gather | solution.py:371
  11.1 11.2 %collective-permute-start = (f32[576,128]{1,0:T(8,128)S(1)}, f32[576,128]{1,0:T(8,128)S(1)}, u32[]{:S(2)}, u32[]{:S(2)}) collective-permute-start(f32[576,128]{1,0:T(8,128)S(1)} %bitcast.12), channel_id=1, source_target_pairs={{0,4},{1,509},{2,6},{3,511},{4,8},{5,1},{6,10},{7,3},{8,12},{9,5},... | collective-permute-start | bytes 884744 | tf_op jit(solution)/shard_map/ppermute | solution.py:360
  22.4 0.0 copy-start
  22.4 3.1 %collective-permute-start.2 = (f32[960,128]{1,0:T(8,128)S(1)}, f32[960,128]{1,0:T(8,128)S(1)}, u32[]{:S(2)}, u32[]{:S(2)}) collective-permute-start(f32[960,128]{1,0:T(8,128)S(1)} %pad_maximum_fusion), channel_id=1, source_target_pairs={{0,2},{1,511},{2,4},{3,1},{4,6},{5,3},{6,8},{7,5},{8,10},{9,7},{10... | collective-permute-start | bytes 1474568 | tf_op jit(solution)/shard_map/ppermute | solution.py:360
  25.5 0.0 copy-done
  25.5 0.3 viscous_part.1.base_ref
  25.8 2.0 %spread.3.refs_1_ = f32[4,384,128]{2,1,0:T(8,128)S(1)} custom-call(f32[504,128]{1,0:T(8,128)S(1)} %get-tuple-element.6.refs_0_), custom_call_target="tpu_custom_call" | custom-call | flops 1610612736 | bytes 2000000 | tf_op jit(solution)/shard_map/spread/pallas_call | solution.py:191
  27.8 1.3 %collective-permute-done.refs_0_ = f32[576,128]{1,0:T(8,128)S(1)} collective-permute-done((f32[576,128]{1,0:T(8,128)S(1)}, f32[576,128]{1,0:T(8,128)S(1)}, u32[]{:S(2)}, u32[]{:S(2)}) %collective-permute-start) | collective-permute-done | bytes 294944 | tf_op jit(solution)/shard_map/ppermute | solution.py:360
  29.2 6.2 %collective-permute-start.1 = (f32[576,128]{1,0:T(8,128)S(1)}, f32[576,128]{1,0:T(8,128)S(1)}, u32[]{:S(2)}, u32[]{:S(2)}) collective-permute-start(f32[576,128]{1,0:T(8,128)S(1)} %collective-permute-done.refs_0_), channel_id=1, source_target_pairs={{0,2},{1,511},{2,4},{3,1},{4,6},{5,3},{6,8},{7,5},{8,10},{9,7},{10... | collective-permute-start | bytes 884744 | tf_op jit(solution)/shard_map/ppermute | solution.py:360
  35.4 4.5 %spread.4.refs_1_ = f32[4,384,128]{2,1,0:T(8,128)S(1)} custom-call(f32[576,128]{1,0:T(8,128)S(1)} %collective-permute-done.refs_0_, f32[4,384,128]{2,1,0:T(8,128)S(1)} %spread.3.refs_1_), custom_call_target="tpu_custom_call", output_to_operand_aliasing={{}: (1, {})} | custom-call | flops 3221225472 | bytes 2000000 | tf_op jit(solution)/shard_map/spread/pallas_call | solution.py:191
  39.9 0.0 collective-permute-done.2.refs_0_.planes_ref
  39.9 4.5 %spread.5.in_ref = f32[4,384,128]{2,1,0:T(8,128)S(1)} custom-call(f32[960,128]{1,0:T(8,128)S(1)} %collective-permute-done.2.refs_0_.planes_ref, f32[4,384,128]{2,1,0:T(8,128)S(1)} %spread.4.refs_1_), custom_call_target="tpu_custom_call", output_to_operand_aliasing={{}: (1, {})} | custom-call | flops 3221225472 | bytes 2000000 | tf_op jit(solution)/shard_map/spread/pallas_call | solution.py:191
  44.4 0.0 collective-permute-done.1.list_ref
  44.4 0.2 spread_last.1
  44.7 2.5 %all-gather.1 = f32[1920,128]{1,0:T(8,128)S(1)} all-gather(f32[960,128]{1,0:T(8,128)S(1)} %get-tuple-element.9), channel_id=3, replica_groups=mesh['gz'=256,'col'=2] {'col'}, dimensions={0}, use_global_device_ids=true | all-gather | bytes 1474560 | tf_op jit(solution)/shard_map/all_gather | solution.py:382
  47.2 0.9 %finish.1 = (f32[4,3,64,128]{3,2,1,0:T(8,128)}, f32[4,3,64,128]{3,2,1,0:T(8,128)}) custom-call(f32[768,128]{1,0:T(8,128)S(1)} %get-tuple-element.8.keep_ref, f32[2,960,128]{2,1,0:T(8,128)S(1)} %bitcast.11, f32[4,3,64,128]{3,2,1,0:T(8,128)S(1)} %viscous_part.1.base_ref, f32[960,128]{1,0:T(8,128)S(1)} %collective-permute-done.2.refs_0_.planes_ref), custom_call_target="tpu_custom_call" | custom-call | tf_op jit(solution)/shard_map/finish/pallas_call | solution.py:297
  (4 shorter events, 0.1 us)
Async XLA Ops:
  11.1 18.1 %collective-permute-start = (f32[576,128]{1,0:T(8,128)S(1)}, f32[576,128]{1,0:T(8,128)S(1)}, u32[]{:S(2)}, u32[]{:S(2)}) collective-permute-start(f32[576,128]{1,0:T(8,128)S(1)} %bitcast.12), channel_id=1, source_target_pairs={{0,4},{1,509},{2,6},{3,511},{4,8},{5,1},{6,10},{7,3},{8,12},{9,5},... | collective-permute-start | bytes 884744 | tf_op jit(solution)/shard_map/ppermute | solution.py:360
  22.4 3.2 %copy-start = (f32[4,3,64,128]{3,2,1,0:T(8,128)S(1)}, f32[4,3,64,128]{3,2,1,0:T(8,128)}, u32[]{:S(2)}) copy-start(f32[4,3,64,128]{3,2,1,0:T(8,128)} %v_ref.3) | copy-start | bytes 1179652
  22.4 17.5 %collective-permute-start.2 = (f32[960,128]{1,0:T(8,128)S(1)}, f32[960,128]{1,0:T(8,128)S(1)}, u32[]{:S(2)}, u32[]{:S(2)}) collective-permute-start(f32[960,128]{1,0:T(8,128)S(1)} %pad_maximum_fusion), channel_id=1, source_target_pairs={{0,2},{1,511},{2,4},{3,1},{4,6},{5,3},{6,8},{7,5},{8,10},{9,7},{10... | collective-permute-start | bytes 1474568 | tf_op jit(solution)/shard_map/ppermute | solution.py:360
  29.2 15.3 %collective-permute-start.1 = (f32[576,128]{1,0:T(8,128)S(1)}, f32[576,128]{1,0:T(8,128)S(1)}, u32[]{:S(2)}, u32[]{:S(2)}) collective-permute-start(f32[576,128]{1,0:T(8,128)S(1)} %collective-permute-done.refs_0_), channel_id=1, source_target_pairs={{0,2},{1,511},{2,4},{3,1},{4,6},{5,3},{6,8},{7,5},{8,10},{9,7},{10... | collective-permute-start | bytes 884744 | tf_op jit(solution)/shard_map/ppermute | solution.py:360
where the time goes:
time: 48.4 us; the launch traced here: 48.1 us
  starting transfers between devices  20.6 us (43%)
  Pallas kernels  13.6 us (28%)
  blocking collectives  11.2 us (23%)
  between operations  1.41 us (3%)
  waiting for transfers between devices  1.33 us (3%)
    ppermute x3, starting transfers between devices, by_core(): return lax.ppermute(x, ('gz', 'col'), pairs)  20.6 us
    pallas_call x3, Pallas kernels, spread(): pl.pallas_call(kernel, out_shape=pltpu.VMEM((depth, 3 * span_x, span_y),...  11 us
    all_gather x1, blocking collectives, on_device(): both = lax.all_gather(sent, 'col', axis=0, tiled=False)  8.64 us
    all_gather x1, blocking collectives, on_device(): given = lax.all_gather(give, 'col', axis=0, tiled=False)  2.51 us
    ppermute x3, waiting for transfers between devices, by_core(): return lax.ppermute(x, ('gz', 'col'), pairs)  1.33 us
    pallas_call x1, Pallas kernels, pack(): pl.pallas_call(kernel, out_shape=(pltpu.VMEM((total, span_y), jnp.float32...  1.15 us
  transfers between devices with their start and end apart: 3, of which 1 were waited for; matrix products, arithmetic and copies ran while one was open for 0% of the time, Pallas kernels for 23%

commit v1 on v0

--- a/solution.py
+++ b/solution.py
@@ -9,8 +9,9 @@
 ROWS = 32
 ATTRS = 9
 LIST = ROWS * ATTRS
-KROWS = 16
+KROWS = 8
 KERNEL_VMEM = 16 << 20
+UNROLL = 4
 SLOTS = 24
 TILE = 16
 
@@ -147,14 +148,13 @@
 
     fill(0, 0)
 
-    def two_turns(i, carry):
-        fill(2 * i + 1, 1)
-        add(0)
-        fill(jnp.minimum(2 * i + 2, turns - 1), 0)
-        add(1)
+    def some_turns(i, carry):
+        for u in range(UNROLL):
+            fill(jnp.minimum(UNROLL * i + u + 1, turns - 1), (u + 1) % 2)
+            add(u % 2)
         return carry
 
-    lax.fori_loop(0, turns // 2, two_turns, 0)
+    lax.fori_loop(0, turns // UNROLL, some_turns, 0)
 
 
 def scratch(lists):

time: 48.4 us -> 47.8 us (0.988)
  Pallas kernels: 13.6 us -> 13.1 us
    pallas_call x3, Pallas kernels: 11 us -> 6.4 us  [spread(): pl.pallas_call(kernel, out_shape=pltpu.VMEM((depth, 3 * span_x, span_y),...]
    pallas_call x1, Pallas kernels: 0.25 us -> 4.34 us  [spread_last(): pl.pallas_call(kernel, out_shape=(pltpu.VMEM((rows, span_y), jnp.float32)...]
  transfers between devices with their start and end apart: 3 -> 3, of which waited for: 1 -> 1; matrix products, arithmetic and copies ran while one was open for 0% -> 0% of each run, Pallas kernels for 23% -> 14%
where the time goes in v1:
time: 47.8 us; the launch traced here: 47.7 us
  starting transfers between devices  20.6 us (43%)
  Pallas kernels  13.1 us (27%)
  blocking collectives  11.2 us (23%)
  between operations  1.41 us (3%)
  waiting for transfers between devices  1.33 us (3%)
    ppermute x3, starting transfers between devices, by_core(): return lax.ppermute(x, ('gz', 'col'), pairs)  20.6 us
    all_gather x1, blocking collectives, on_device(): both = lax.all_gather(sent, 'col', axis=0, tiled=False)  8.64 us
    pallas_call x3, Pallas kernels, spread(): pl.pallas_call(kernel, out_shape=pltpu.VMEM((depth, 3 * span_x, span_y),...  6.4 us
    pallas_call x1, Pallas kernels, spread_last(): pl.pallas_call(kernel, out_shape=(pltpu.VMEM((rows, span_y), jnp.float32)...  4.34 us
    all_gather x1, blocking collectives, on_device(): given = lax.all_gather(give, 'col', axis=0, tiled=False)  2.51 us
    ppermute x3, waiting for transfers between devices, by_core(): return lax.ppermute(x, ('gz', 'col'), pairs)  1.33 us
    pallas_call x1, Pallas kernels, pack(): pl.pallas_call(kernel, out_shape=(pltpu.VMEM((total, span_y), jnp.float32...  1.15 us
  transfers between devices with their start and end apart: 3, of which 1 were waited for; matrix products, arithmetic and copies ran while one was open for 0% of the time, Pallas kernels for 14%

profile of v1, /device:TPU:1, one launch (start us, length us, event | category | flops | bytes accessed | tf_op | source)
XLA Modules:
  0.0 47.7 jit_solution(17262998966312283294)
XLA Ops:
  1.3 1.2 %pack.1 = (f32[504,128]{1,0:T(8,128)S(1)}, f32[192,128]{1,0:T(8,128)S(1)}) custom-call(s32[1]{0:T(128)S(6)} %copy.13.start_ref, f32[4,3,64,128]{3,2,1,0:T(8,128)} %v_ref.3, f32[3,4096]{1,0:T(4,128)} %f_ref.1, f32[3,4096]{1,0:T(4,128)} %o_ref.1, s32[32,128]{1,0:T(8,128)} %bitcast.14, s32[32,128]{1,0:T(8,128)} %bitcast.15, s32[32,128]{1,0:T(8,128)} %bitcast.16), custom_call_target="tpu_custom_call" | custom-call | tf_op jit(solution)/shard_map/pack/pallas_call | solution.py:335
  2.4 8.6 %all-gather = f32[1008,128]{1,0:T(8,128)S(1)} all-gather(f32[504,128]{1,0:T(8,128)S(1)} %get-tuple-element.6.refs_0_), channel_id=2, replica_groups=mesh['gz'=256,'col'=2] {'col'}, dimensions={0}, use_global_device_ids=true | all-gather | bytes 774144 | tf_op jit(solution)/shard_map/all_gather | solution.py:371
  11.1 11.2 %collective-permute-start = (f32[576,128]{1,0:T(8,128)S(1)}, f32[576,128]{1,0:T(8,128)S(1)}, u32[]{:S(2)}, u32[]{:S(2)}) collective-permute-start(f32[576,128]{1,0:T(8,128)S(1)} %bitcast.12), channel_id=1, source_target_pairs={{0,4},{1,509},{2,6},{3,511},{4,8},{5,1},{6,10},{7,3},{8,12},{9,5},... | collective-permute-start | bytes 884744 | tf_op jit(solution)/shard_map/ppermute | solution.py:360
  22.4 0.0 copy-start
  22.4 3.1 %collective-permute-start.2 = (f32[960,128]{1,0:T(8,128)S(1)}, f32[960,128]{1,0:T(8,128)S(1)}, u32[]{:S(2)}, u32[]{:S(2)}) collective-permute-start(f32[960,128]{1,0:T(8,128)S(1)} %pad_maximum_fusion), channel_id=1, source_target_pairs={{0,2},{1,511},{2,4},{3,1},{4,6},{5,3},{6,8},{7,5},{8,10},{9,7},{10... | collective-permute-start | bytes 1474568 | tf_op jit(solution)/shard_map/ppermute | solution.py:360
  25.5 0.0 copy-done
  25.5 0.3 viscous_part.1.base_ref
  25.8 2.0 %spread.3.refs_1_ = f32[4,384,128]{2,1,0:T(8,128)S(1)} custom-call(f32[504,128]{1,0:T(8,128)S(1)} %get-tuple-element.6.refs_0_), custom_call_target="tpu_custom_call" | custom-call | flops 1610612736 | bytes 2000000 | tf_op jit(solution)/shard_map/spread/pallas_call | solution.py:191
  27.8 1.3 %collective-permute-done.refs_0_ = f32[576,128]{1,0:T(8,128)S(1)} collective-permute-done((f32[576,128]{1,0:T(8,128)S(1)}, f32[576,128]{1,0:T(8,128)S(1)}, u32[]{:S(2)}, u32[]{:S(2)}) %collective-permute-start) | collective-permute-done | bytes 294944 | tf_op jit(solution)/shard_map/ppermute | solution.py:360
  29.2 6.2 %collective-permute-start.1 = (f32[576,128]{1,0:T(8,128)S(1)}, f32[576,128]{1,0:T(8,128)S(1)}, u32[]{:S(2)}, u32[]{:S(2)}) collective-permute-start(f32[576,128]{1,0:T(8,128)S(1)} %collective-permute-done.refs_0_), channel_id=1, source_target_pairs={{0,2},{1,511},{2,4},{3,1},{4,6},{5,3},{6,8},{7,5},{8,10},{9,7},{10... | collective-permute-start | bytes 884744 | tf_op jit(solution)/shard_map/ppermute | solution.py:360
  35.4 0.1 spread.4.refs_1_
  35.6 0.0 collective-permute-done.2.refs_0_.planes_ref
  35.6 4.2 %spread.5.in_ref = f32[4,384,128]{2,1,0:T(8,128)S(1)} custom-call(f32[960,128]{1,0:T(8,128)S(1)} %collective-permute-done.2.refs_0_.planes_ref, f32[4,384,128]{2,1,0:T(8,128)S(1)} %spread.4.refs_1_), custom_call_target="tpu_custom_call", output_to_operand_aliasing={{}: (1, {})} | custom-call | flops 3221225472 | bytes 2000000 | tf_op jit(solution)/shard_map/spread/pallas_call | solution.py:191
  39.8 0.0 collective-permute-done.1.list_ref
  39.8 4.3 %spread_last.1 = (f32[768,128]{1,0:T(8,128)S(1)}, f32[960,128]{1,0:T(8,128)S(1)}) custom-call(f32[576,128]{1,0:T(8,128)S(1)} %collective-permute-done.1.list_ref, f32[4,384,128]{2,1,0:T(8,128)S(1)} %spread.5.in_ref, f32[960,128]{1,0:T(8,128)S(1)} %collective-permute-done.2.refs_0_.planes_ref), custom_call_target="tpu_custom_call" | custom-call | flops 3221225472 | bytes 2000000 | tf_op jit(solution)/shard_map/spread_last/pallas_call | solution.py:222
  44.2 2.5 %all-gather.1 = f32[1920,128]{1,0:T(8,128)S(1)} all-gather(f32[960,128]{1,0:T(8,128)S(1)} %get-tuple-element.9), channel_id=3, replica_groups=mesh['gz'=256,'col'=2] {'col'}, dimensions={0}, use_global_device_ids=true | all-gather | bytes 1474560 | tf_op jit(solution)/shard_map/all_gather | solution.py:382
  46.7 0.9 %finish.1 = (f32[4,3,64,128]{3,2,1,0:T(8,128)}, f32[4,3,64,128]{3,2,1,0:T(8,128)}) custom-call(f32[768,128]{1,0:T(8,128)S(1)} %get-tuple-element.8.keep_ref, f32[2,960,128]{2,1,0:T(8,128)S(1)} %bitcast.11, f32[4,3,64,128]{3,2,1,0:T(8,128)S(1)} %viscous_part.1.base_ref, f32[960,128]{1,0:T(8,128)S(1)} %collective-permute-done.2.refs_0_.planes_ref), custom_call_target="tpu_custom_call" | custom-call | tf_op jit(solution)/shard_map/finish/pallas_call | solution.py:297
  (4 shorter events, 0.1 us)
Async XLA Ops:
  11.1 18.1 %collective-permute-start = (f32[576,128]{1,0:T(8,128)S(1)}, f32[576,128]{1,0:T(8,128)S(1)}, u32[]{:S(2)}, u32[]{:S(2)}) collective-permute-start(f32[576,128]{1,0:T(8,128)S(1)} %bitcast.12), channel_id=1, source_target_pairs={{0,4},{1,509},{2,6},{3,511},{4,8},{5,1},{6,10},{7,3},{8,12},{9,5},... | collective-permute-start | bytes 884744 | tf_op jit(solution)/shard_map/ppermute | solution.py:360
  22.4 3.2 %copy-start = (f32[4,3,64,128]{3,2,1,0:T(8,128)S(1)}, f32[4,3,64,128]{3,2,1,0:T(8,128)}, u32[]{:S(2)}) copy-start(f32[4,3,64,128]{3,2,1,0:T(8,128)} %v_ref.3) | copy-start | bytes 1179652
  22.4 13.2 %collective-permute-start.2 = (f32[960,128]{1,0:T(8,128)S(1)}, f32[960,128]{1,0:T(8,128)S(1)}, u32[]{:S(2)}, u32[]{:S(2)}) collective-permute-start(f32[960,128]{1,0:T(8,128)S(1)} %pad_maximum_fusion), channel_id=1, source_target_pairs={{0,2},{1,511},{2,4},{3,1},{4,6},{5,3},{6,8},{7,5},{8,10},{9,7},{10... | collective-permute-start | bytes 1474568 | tf_op jit(solution)/shard_map/ppermute | solution.py:360
  29.2 10.7 %collective-permute-start.1 = (f32[576,128]{1,0:T(8,128)S(1)}, f32[576,128]{1,0:T(8,128)S(1)}, u32[]{:S(2)}, u32[]{:S(2)}) collective-permute-start(f32[576,128]{1,0:T(8,128)S(1)} %collective-permute-done.refs_0_), channel_id=1, source_target_pairs={{0,2},{1,511},{2,4},{3,1},{4,6},{5,3},{6,8},{7,5},{8,10},{9,7},{10... | collective-permute-start | bytes 884744 | tf_op jit(solution)/shard_map/ppermute | solution.py:360
